TPU v7x, 256 devices: a whole 4x4x8 slice. The times are simulated.
256 devices in a mesh: dp: 32 (over z_hi, y, core), mp: 8 (over z_lo, x).
Axes of the slice: x: 4, y: 4, z: 8 (z_hi: 4, z_lo: 2; z = z_hi * 2 + z_lo), core: 2. Of those that a mesh axis runs over, the one named last changes fastest.
Arguments:
- features: bfloat16 [4096, 4608], P('dp'), may hold values from -6 to 6
- proj_in: bfloat16 [4608, 2560], P('dp', 'mp'), may hold values from -0.09375 to 0.09375
- proj_out: bfloat16 [2560, 2560], P('mp'), may hold values from -0.125 to 0.125
- expert_gate: bfloat16 [64, 2560, 1536], P('dp', None, 'mp'), may hold values from -0.125 to 0.125
- expert_up: bfloat16 [64, 2560, 1536], P('dp', None, 'mp'), may hold values from -0.125 to 0.125
- expert_down: bfloat16 [64, 1536, 2560], P('dp', 'mp'), may hold values from -0.15625 to 0.15625
- routes: int32 [4096, 6], P('dp'), may hold values from 0 to 63, all different within a row; in each aligned block of 128 rows (0 to 127, 128 to 255, ...) at most 15 rows name the same one
- gate_weights: float32 [4096, 6], P('dp'), may hold values from 0.1 to 0.6
- cotangent: bfloat16 [4096, 2560], P('dp'), may hold values from -0.09375 to 0.09375
- first_in: float32 [4608, 2560], P('dp', 'mp'), may hold values from -2 to 2
- second_in: float32 [4608, 2560], P('dp', 'mp'), may hold values from 0.02 to 1
- first_out: float32 [2560, 2560], P('mp', 'dp'), may hold values from -2 to 2
- second_out: float32 [2560, 2560], P('mp', 'dp'), may hold values from 0.02 to 1
Outputs:
- moe_out: bfloat16 [4096, 2560], P('dp')
- new_proj_in: bfloat16 [4608, 2560], P('dp', 'mp')
- new_proj_out: bfloat16 [2560, 2560], P('mp', 'dp')
- new_first_in: float32 [4608, 2560], P('dp', 'mp')
- new_second_in: float32 [4608, 2560], P('dp', 'mp')
- new_first_out: float32 [2560, 2560], P('mp', 'dp')
- new_second_out: float32 [2560, 2560], P('mp', 'dp')
Inputs may be any that keep to these rules, and one draw needn't show every extreme that they name: `routes`: each row names 6 different experts. Within the rows of one device (aligned blocks of 128 rows) no expert is named more than 15 times, and in every draw some expert is named exactly 15 times in some block.
All inputs are finite; a program needn't handle non-finite values.
Results may differ from a plain program's by a relative error of at most 0.01.
Values may be sent and summed in bfloat16 or wider, within the bound.
No kernel may reach another device: no remote copies, remote signals or barrier semaphores. Data moves between devices by JAX's collectives and lax.ppermute only.
A program may use at most 128 MiB of HBM per device.

v0:
```python
import jax
import jax.numpy as jnp
from jax import lax
from jax.sharding import PartitionSpec as P

EXPERTS = 64
TOP = 6
CAP = 15
BETA_ONE = 0.9
BETA_TWO = 0.999
EPSILON = 1e-08
LEARN_RATE = 0.001
WEIGHT_DECAY = 0.1
FIRST_FIX = 1.0 - 0.9**50 * 0.9**50
SECOND_FIX = 1.0 - 0.999**50 * 0.999**50


def in_blocks(value, dim, peers):
    before, after = (value.shape[:dim], value.shape[dim + 1 :])
    return jnp.moveaxis(value.reshape(*before, peers, -1, *after), dim, 0)


def sent_and_summed(value, axis, dim):
    pieces = in_blocks(value, dim, lax.axis_size(axis))
    arrived = lax.all_to_all(pieces, axis, split_axis=0, concat_axis=0, tiled=True)
    return arrived.sum(axis=0)


def sent_together(arrays, axis, split_dim, concat_dim, along):
    widths = [a.shape[along] for a in arrays]
    both = jnp.concatenate(arrays, axis=along)
    out = lax.all_to_all(both, axis, split_axis=split_dim, concat_axis=concat_dim, tiled=True)
    return tuple(jnp.split(out, [sum(widths[:k]) for k in range(1, len(widths))], axis=along))


def sent_together_2(arrays, axis, dim, along):
    both = jnp.concatenate(arrays, axis=along)
    out, at, done = (lax.psum_scatter(both, axis, scatter_dimension=dim, tiled=True), 0, [])
    for a in arrays:
        done.append(lax.slice_in_dim(out, at, at + a.shape[along], axis=along))
        at += a.shape[along]
    return tuple(done)


def turned_gather(arrays, axis, dims):
    turned = [jnp.moveaxis(a, dim, 0) for a, dim in zip(arrays, dims)]
    widths = [t[0].size for t in turned]
    both = jnp.concatenate([t.reshape(-1, w) for t, w in zip(turned, widths)], axis=1)
    out = lax.all_gather(both, axis, axis=0, tiled=True)
    pieces = jnp.split(out, [sum(widths[:k]) for k in range(1, len(widths))], axis=1)
    return tuple(
        (
            jnp.moveaxis(b.reshape(-1, *t.shape[1:]), 0, dim)
            for b, t, dim in zip(pieces, turned, dims)
        )
    )


def gelu_parts(preact):

    def smooth(values):
        return jax.nn.gelu(values, approximate=True)

    result, pullback = jax.vjp(smooth, preact)
    return (result, pullback(jnp.ones_like(preact))[0])


def slot_table(chosen_block):
    chosen = chosen_block.reshape(-1)
    onehot = (chosen[:, None] == jnp.arange(EXPERTS, dtype=jnp.int32)[None, :]).astype(jnp.int32)
    earlier = jnp.cumsum(onehot, axis=0) - onehot
    return (chosen, jnp.sum(earlier * onehot, axis=1))


def adamw_update(weight, gradient, first, second):
    first_new = BETA_ONE * first + (1.0 - BETA_ONE) * gradient
    second_new = BETA_TWO * second + (1.0 - BETA_TWO) * gradient * gradient
    update = first_new / FIRST_FIX / (jnp.sqrt(second_new / SECOND_FIX) + EPSILON)
    current = weight.astype(jnp.float32)
    return (
        (current - LEARN_RATE * (update + WEIGHT_DECAY * current)).astype(jnp.bfloat16),
        first_new,
        second_new,
    )


def expert_pass(inputs, grads_in, w_gate, w_up, w_down):
    gate_projection = jnp.einsum("erd,edf->erf", inputs, w_gate, preferred_element_type=jnp.float32)
    up_projection = jnp.einsum("erd,edf->erf", inputs, w_up, preferred_element_type=jnp.float32)
    sigmoid_gate = jax.nn.sigmoid(gate_projection)
    silu_gate = gate_projection * sigmoid_gate
    inner_activation = (silu_gate * up_projection).astype(jnp.bfloat16)
    out_part = jnp.einsum(
        "erf,efd->erd", inner_activation, w_down, preferred_element_type=jnp.float32
    ).astype(jnp.bfloat16)
    down_weight_gradient = jnp.einsum(
        "erd,efd->erf", grads_in, w_down, preferred_element_type=jnp.float32
    )
    gate_weight_gradient = (
        down_weight_gradient
        * up_projection
        * sigmoid_gate
        * (1.0 + gate_projection * (1.0 - sigmoid_gate))
    ).astype(jnp.bfloat16)
    up_weight_gradient = (down_weight_gradient * silu_gate).astype(jnp.bfloat16)
    input_part = (
        jnp.einsum("erf,edf->erd", gate_weight_gradient, w_gate, preferred_element_type=jnp.float32)
        + jnp.einsum("erf,edf->erd", up_weight_gradient, w_up, preferred_element_type=jnp.float32)
    ).astype(jnp.bfloat16)
    return (out_part, input_part)


def slot_sources(position, flat_weights, total_slots):
    pair_count = position.shape[0]
    owner = (
        jnp.zeros((total_slots,), jnp.int32)
        .at[position]
        .set(jnp.arange(pair_count, dtype=jnp.int32) + 1)
    )
    live = owner > 0
    pair_id = jnp.maximum(owner - 1, 0)
    source_row = pair_id // TOP
    slot_weight = jnp.where(live, flat_weights[pair_id], 0.0)
    return (live, source_row, slot_weight)


def fill_inputs(rows, live, source_row):
    return jnp.where(live[:, None], rows[source_row], jnp.zeros((), rows.dtype))


def fill_grads(grads, slot_weight, source_row):
    return (slot_weight[:, None] * grads[source_row].astype(jnp.float32)).astype(jnp.bfloat16)


def collect_rows(buffer, pair_slots, pair_weights):
    flat = buffer.reshape(-1, buffer.shape[-1])
    total = jnp.zeros((pair_slots.shape[0], flat.shape[1]), jnp.float32)
    for choice_index in range(TOP):
        picked = flat[pair_slots[:, choice_index]]
        if pair_weights is None:
            total = total + picked
        else:
            total = total + pair_weights[:, choice_index : choice_index + 1] * picked
    return total


def local(
    features,
    proj_in,
    proj_out,
    expert_gate,
    expert_up,
    expert_down,
    routes,
    gate_weights,
    cotangent,
    first_in,
    second_in,
    first_out,
    second_out,
):
    row_count = features.shape[0]
    model_width = cotangent.shape[1]
    data_parts = lax.axis_size("dp")
    model_parts = lax.axis_size("mp")
    data_place = lax.axis_index("dp")
    model_place = lax.axis_index("mp")
    column_width = model_width // model_parts
    column_start = model_place * column_width
    own_experts = expert_gate.shape[0]
    total_slots = own_experts * data_parts * CAP
    expert_rows = data_parts * CAP
    preact = jnp.dot(
        features,
        lax.all_gather(proj_in, "dp", axis=0, tiled=True),
        preferred_element_type=jnp.float32,
    )
    activated, gelu_slope = gelu_parts(preact)
    hidden = activated.astype(jnp.bfloat16)
    partial_value = jnp.dot(hidden, proj_out, preferred_element_type=jnp.float32)
    chosen, slot_index = slot_table(routes)
    position = chosen * CAP + slot_index
    pair_slots = position.reshape(row_count, TOP)
    live, source_row, slot_weight = slot_sources(position, gate_weights.reshape(-1), total_slots)
    cotangent_cols = lax.dynamic_slice_in_dim(cotangent, column_start, column_width, 1)
    mapped_cols = sent_and_summed(partial_value, "mp", 1).astype(jnp.bfloat16)
    send_rows = fill_inputs(mapped_cols, live, source_row)
    send_grads = fill_grads(cotangent_cols, slot_weight, source_row)
    send_shape = (data_parts, own_experts, CAP, column_width)
    narrow_rows, narrow_grads = sent_together(
        (send_rows.reshape(send_shape), send_grads.reshape(send_shape)), "dp", 0, 2, 1
    )
    recv_rows, recv_grads = (
        lax.all_gather(narrow_rows, "mp", axis=3, tiled=True),
        lax.all_gather(narrow_grads, "mp", axis=3, tiled=True),
    )
    out_part, input_part = expert_pass(
        recv_rows.reshape(own_experts, expert_rows, model_width),
        recv_grads.reshape(own_experts, expert_rows, model_width),
        expert_gate,
        expert_up,
        expert_down,
    )
    back_shape = (1, own_experts, expert_rows, model_width)
    summed_out, summed_in = tuple(
        (
            part.astype(jnp.float32)
            for part in sent_together_2(
                (
                    out_part.astype(jnp.float32).reshape(back_shape).astype(jnp.bfloat16),
                    input_part.astype(jnp.float32).reshape(back_shape).astype(jnp.bfloat16),
                ),
                "mp",
                3,
                0,
            )
        )
    )
    back_out, back_in = sent_together((summed_out, summed_in), "dp", 2, 0, 1)
    moe_cols = (
        mapped_cols.astype(jnp.float32) + collect_rows(back_out, pair_slots, gate_weights)
    ).astype(jnp.bfloat16)
    grad_cols = (
        cotangent_cols.astype(jnp.float32) + collect_rows(back_in, pair_slots, None)
    ).astype(jnp.bfloat16)
    moe_out, grad_mapped = turned_gather((moe_cols, grad_cols), "mp", (1, 1))
    grad_hidden = lax.dot_general(
        grad_mapped, proj_out, (((1,), (1,)), ((), ())), preferred_element_type=jnp.float32
    )
    grad_pre = (grad_hidden * gelu_slope).astype(jnp.bfloat16)
    vis_part = features.shape[1] // data_parts
    width_part = model_width // data_parts
    share_rows = vis_part + width_part
    feature_blocks = features.reshape(row_count, data_parts, vis_part)
    mapped_blocks = grad_mapped.reshape(row_count, data_parts, width_part)
    term_in = jnp.einsum(
        "tnv,th->nvh", feature_blocks, grad_pre, preferred_element_type=jnp.float32
    )
    term_out = jnp.einsum("tnd,th->ndh", mapped_blocks, hidden, preferred_element_type=jnp.float32)
    shares = lax.psum_scatter(
        jnp.concatenate([term_in, term_out], axis=1)
        .reshape(share_rows * lax.axis_size("dp"), hidden.shape[1])
        .astype(jnp.bfloat16),
        "dp",
        scatter_dimension=0,
        tiled=True,
    ).astype(jnp.float32)
    grad_in = shares[:vis_part]
    grad_out = shares[vis_part:].T
    own_out = lax.dynamic_slice_in_dim(proj_out, data_place * width_part, width_part, 1)
    new_in, first_in_new, second_in_new = adamw_update(proj_in, grad_in, first_in, second_in)
    new_out, first_out_new, second_out_new = adamw_update(own_out, grad_out, first_out, second_out)
    return (moe_out, new_in, new_out, first_in_new, second_in_new, first_out_new, second_out_new)


def solution(mesh):
    return jax.shard_map(
        local,
        mesh=mesh,
        in_specs=(
            P("dp", None),
            P("dp", "mp"),
            P("mp", None),
            P("dp", None, "mp"),
            P("dp", None, "mp"),
            P("dp", "mp", None),
            P("dp", None),
            P("dp", None),
            P("dp", None),
            P("dp", "mp"),
            P("dp", "mp"),
            P("mp", "dp"),
            P("mp", "dp"),
        ),
        out_specs=(
            P("dp", None),
            P("dp", "mp"),
            P("mp", "dp"),
            P("dp", "mp"),
            P("dp", "mp"),
            P("mp", "dp"),
            P("mp", "dp"),
        ),
        check_vma=False,
    )
```

profile of v0, /device:TPU:2, one launch (start us, length us, event | category | flops | bytes accessed | tf_op | source)
XLA Modules:
  0.0 869.0 jit_solution(17863692709619640517)
XLA Ops:
  7.9 64.8 %all-gather.5.cloned.1.call-done = bf16[4608,320]{1,0:T(8,128)(2,1)} async-done(((bf16[144,320]{1,0:T(8,128)(2,1)}), bf16[4608,320]{1,0:T(8,128)(2,1)}) %all-gather.5.cloned.1.call-update) | async-done | bytes 2949136 | tf_op jit(solution)/shard_map/all_gather | solution.py:175
  72.7 3.9 fusion.81
  76.6 2.0 fusion.73
  78.6 4.9 all-to-all-start
  84.0 1.8 reduce-window.6
  87.2 3.4 scatter_custom_fusion
  91.6 5.0 gather_fusion.2
  100.3 4.8 gather_fusion.1
  106.5 1.4 broadcast_in_dim.22
  107.9 1.8 multiply_convert_fusion
  111.3 5.0 gather_fusion
  116.3 1.5 gather.48
  119.8 38.4 %all_to_all.41 = bf16[32,4,15,320]{3,1,2,0:T(4,128)(2,1)S(1)} all-to-all(bf16[32,4,15,320]{3,1,2,0:T(4,128)(2,1)S(1)} %copy.84), channel_id=1, replica_groups=mesh['dp'=32,'mp'=8] {'dp'}, dimensions={0} | all-to-all | bytes 2457600 | tf_op jit(solution)/shard_map/all_to_all | solution.py:32
  159.3 2.2 copy.85
  161.6 2.3 copy.87
  164.2 61.7 %all-gather.7.cloned.1.call-done = bf16[1,2,480,2560]{2,1,0,3:T(2,128)(2,1)} async-done(((bf16[1,2,480,320]{2,1,0,3:T(2,128)(2,1)}), bf16[1,2,480,2560]{2,1,0,3:T(2,128)(2,1)}) %all-gather.7.cloned.1.call-update) | async-done | bytes 4915216 | tf_op jit(solution)/shard_map/all_gather | solution.py:194
  225.9 13.7 %copy.86 = bf16[1,2,480,2560]{3,2,1,0:T(8,128)(2,1)} copy(bf16[1,2,480,2560]{2,1,0,3:T(2,128)(2,1)} %all-gather.7.cloned.1.call-done) | data formatting | bytes 9830400 | tf_op jit(solution)/shard_map/all_gather | solution.py:194
  239.7 4.8 fusion.4
  244.8 2.4 fusion.2
  247.2 44.2 %all-gather.9.cloned.1.call-done = bf16[1,2,480,2560]{2,1,0,3:T(2,128)(2,1)} async-done(((bf16[1,2,480,320]{2,1,0,3:T(2,128)(2,1)}), bf16[1,2,480,2560]{2,1,0,3:T(2,128)(2,1)}) %all-gather.9.cloned.1.call-update) | async-done | bytes 4915216 | tf_op jit(solution)/shard_map/all_gather | solution.py:195
  291.4 13.8 %copy.88 = bf16[1,2,480,2560]{3,2,1,0:T(8,128)(2,1)} copy(bf16[1,2,480,2560]{2,1,0,3:T(2,128)(2,1)} %all-gather.9.cloned.1.call-done) | data formatting | bytes 9830400 | tf_op jit(solution)/shard_map/all_gather | solution.py:195
  305.2 4.0 fusion
  309.2 3.7 fusion.6
  313.0 1.5 fusion.11
  314.5 3.7 fusion.7
  318.2 8.4 pad_maximum_fusion
  326.7 26.2 %copy.89 = bf16[2,2,480,2560]{2,1,0,3:T(2,128)(2,1)} copy(bf16[2,2,480,2560]{3,2,1,0:T(8,128)(2,1)} %pad_maximum_fusion) | data formatting | bytes 19660800 | tf_op jit(solution)/shard_map/concatenate | solution.py:37
  354.8 226.2 %all-reduce.3.cloned.1.call-done = bf16[2,2,480,2560]{2,1,0,3:T(2,128)(2,1)} async-done(((bf16[2,2,480,2560]{2,1,0,3:T(2,128)(2,1)}), bf16[2,2,480,2560]{2,1,0,3:T(2,128)(2,1)}) %all-reduce.3.cloned.1.call-update) | async-done | bytes 9830416
  581.0 2.2 constant_dynamic-slice_fusion
  583.4 1.7 maximum_convert_fusion
  585.1 4.4 copy.92
  589.5 10.1 %all-to-all-start.2 = ((f32[1,4,480,320]{3,1,0,2:T(4,128)}), f32[1,4,480,320]{3,1,0,2:T(4,128)}, u32[]{:S(2)}, u32[]{:S(2)}) async-start(f32[1,4,480,320]{3,1,0,2:T(4,128)} %copy.92), calls=%async_computation.2 | async-start | bytes 5898240 | tf_op jit(solution)/shard_map/all_to_all | solution.py:32
  600.7 68.1 %all-to-all-done.2 = f32[1,4,480,320]{3,1,0,2:T(4,128)} async-done(((f32[1,4,480,320]{3,1,0,2:T(4,128)}), f32[1,4,480,320]{3,1,0,2:T(4,128)}, u32[]{:S(2)}, u32[]{:S(2)}) %all-to-all-start.2) | async-done | bytes 2457632 | tf_op jit(solution)/shard_map/all_to_all | solution.py:32
  668.9 4.0 fusion.78
  674.2 1.5 reshape.116
  680.0 1.5 reshape.115
  685.9 1.4 gather_fusion.11
  688.7 1.4 gather_fusion.10
  690.2 1.4 gather_fusion.4
  691.6 1.4 gather_fusion.9
  693.9 1.5 fusion.44
  696.5 37.9 %all-gather.11.cloned.1.call-done = bf16[2560,256]{1,0:T(8,128)(2,1)} async-done(((bf16[320,256]{1,0:T(8,128)(2,1)}), bf16[2560,256]{1,0:T(8,128)(2,1)}) %all-gather.11.cloned.1.call-update) | async-done | bytes 1310736 | tf_op jit(solution)/shard_map/all_gather | solution.py:49
  734.4 2.2 fusion.80
  737.8 6.9 fusion.9
  744.7 3.4 convert_bitcast_fusion
  748.1 3.0 pad_maximum_fusion.1
  753.6 105.0 %reduce-scatter.2.cloned.1.call-done = bf16[224,320]{1,0:T(8,128)(2,1)} async-done(((bf16[7168,320]{1,0:T(8,128)(2,1)}), bf16[224,320]{1,0:T(8,128)(2,1)}) %reduce-scatter.2.cloned.1.call-update) | async-done | bytes 143376 | tf_op jit(solution)/shard_map/reduce_scatter | solution.py:240
  860.5 1.7 fusion.41
  (123 shorter events, 35.1 us)
Async XLA Ops:
  7.2 298.0 %copy-start = (bf16[2,192,2560]{2,1,0:T(8,128)(2,1)S(1)}, bf16[2,192,2560]{2,1,0:T(8,128)(2,1)}, u32[]{:S(2)}) copy-start(bf16[2,192,2560]{2,1,0:T(8,128)(2,1)} %param.18) | copy-start | bytes 5898244
  7.2 65.5 %all-gather.5.cloned.1.call-start = ((), (), s32[]{:S(2)}) async-start(), calls=%async_computation.4 | async-start | bytes 3649536 | tf_op jit(solution)/shard_map/all_gather | solution.py:175
  72.7 3.9 copy-start.7
  76.6 2.0 copy-start.12
  78.6 4.9 copy-start.24
  78.6 31.2 %all-to-all-start = ((f32[8,128,320]{1,2,0:T(8,128)}), f32[8,128,320]{1,2,0:T(8,128)}, u32[]{:S(2)}, u32[]{:S(2)}) async-start(f32[8,128,320]{1,2,0:T(8,128)} %bitcast.1), calls=%async_computation | async-start | bytes 2621440 | tf_op jit(solution)/shard_map/all_to_all | solution.py:25
  83.5 142.4 %all-gather.7.cloned.1.call-start = ((), (), s32[]{:S(2)}) async-start(), calls=%async_computation.5 | async-start | bytes 5898240 | tf_op jit(solution)/shard_map/all_gather | solution.py:194
  96.6 1.4 copy-start.22
  111.3 6.5 copy-start.21
  117.8 1.1 copy-start.10
  161.6 129.9 %all-gather.9.cloned.1.call-start = ((), (), s32[]{:S(2)}) async-start(), calls=%async_computation.6 | async-start | bytes 5898240 | tf_op jit(solution)/shard_map/all_gather | solution.py:195
  163.9 417.1 %all-reduce.3.cloned.1.call-start = ((), (), s32[]{:S(2)}) async-start(), calls=%async_computation.9 | async-start | bytes 20971520
  239.6 4.8 copy-start.2
  239.7 5.2 copy-start.4
  305.2 4.0 copy-start.6
  309.2 3.7 copy-start.3
  313.0 1.6 copy-start.5
  352.9 0.7 copy-start.27
  589.5 10.4 %copy-start.9 = (s32[128,6]{1,0:T(8,128)S(1)}, s32[128,6]{1,0:T(8,128)}, u32[]{:S(2)}) copy-start(s32[128,6]{1,0:T(8,128)} %get-tuple-element.43) | copy-start | bytes 9220
  589.5 10.7 %copy-start.23 = (f32[128,6]{0,1:T(8,128)S(1)}, f32[128,6]{0,1:T(8,128)}, u32[]{:S(2)}) copy-start(f32[128,6]{0,1:T(8,128)} %param.20) | copy-start | bytes 9220
  589.5 79.4 %all-to-all-start.2 = ((f32[1,4,480,320]{3,1,0,2:T(4,128)}), f32[1,4,480,320]{3,1,0,2:T(4,128)}, u32[]{:S(2)}, u32[]{:S(2)}) async-start(f32[1,4,480,320]{3,1,0,2:T(4,128)} %copy.92), calls=%async_computation.2 | async-start | bytes 5898240 | tf_op jit(solution)/shard_map/all_to_all | solution.py:32
  599.6 134.8 %all-gather.11.cloned.1.call-start = ((), (), s32[]{:S(2)}) async-start(), calls=%async_computation.7 | async-start | bytes 1474560 | tf_op jit(solution)/shard_map/all_gather | solution.py:49
  693.1 2.3 copy-start.14
  693.1 2.3 copy-start.15
  693.1 2.3 copy-start.16
  693.1 2.3 copy-start.25
  693.1 2.3 copy-start.26
  695.6 41.0 %copy-start.13 = (f32[128,320]{0,1:T(8,128)S(1)}, f32[128,320]{0,1:T(8,128)}, u32[]{:S(2)}) copy-start(f32[128,320]{0,1:T(8,128)} %copy-done.12) | copy-start | bytes 491524
  696.4 162.2 %reduce-scatter.2.cloned.1.call-start = ((), (), s32[]{:S(2)}) async-start(), calls=%async_computation.8 | async-start | bytes 5677056 | tf_op jit(solution)/shard_map/reduce_scatter | solution.py:240
  736.6 1.3 copy-start.8
  751.1 1.3 copy-start.11
  751.2 108.4 %copy-start.17 = (bf16[144,320]{1,0:T(8,128)(2,1)S(1)}, bf16[144,320]{1,0:T(8,128)(2,1)}, u32[]{:S(2)}) copy-start(bf16[144,320]{1,0:T(8,128)(2,1)} %param.14) | copy-start | bytes 276484
  751.2 108.4 %copy-start.18 = (f32[144,320]{1,0:T(8,128)S(1)}, f32[144,320]{1,0:T(8,128)}, u32[]{:S(2)}) copy-start(f32[144,320]{1,0:T(8,128)} %param.22) | copy-start | bytes 552964
  751.2 108.4 %copy-start.19 = (f32[144,320]{1,0:T(8,128)S(1)}, f32[144,320]{1,0:T(8,128)}, u32[]{:S(2)}) copy-start(f32[144,320]{1,0:T(8,128)} %param.23) | copy-start | bytes 552964
  751.2 109.3 %copy-start.20 = (f32[320,80]{0,1:T(8,128)S(1)}, f32[320,80]{0,1:T(8,128)}, u32[]{:S(2)}) copy-start(f32[320,80]{0,1:T(8,128)} %param.24) | copy-start | bytes 307204
  752.3 109.8 %copy-start.1 = (bf16[2,192,2560]{2,1,0:T(8,128)(2,1)S(1)}, bf16[2,192,2560]{2,1,0:T(8,128)(2,1)}, u32[]{:S(2)}) copy-start(bf16[2,192,2560]{2,1,0:T(8,128)(2,1)} %param.18) | copy-start | bytes 5898244
Sparse Core Ops, SparseCore 0:
  10.6 62.0 all-gather.4
  161.7 64.1 all-gather.6
  227.7 63.6 all-gather.8
  353.1 227.9 all-reduce.2
  696.6 37.7 all-gather.10
  751.3 107.2 reduce-scatter.1
where the time goes:
time: 871 us; the launch traced here: 869 us
  waiting for transfers between devices  609 us (70%)
  local copies, waits for them, and re-layouts  128 us (15%)
  blocking collectives  38.4 us (4%)
  matrix products  33.6 us (4%)
  other arithmetic  29.7 us (3%)
  starting transfers between devices  15.6 us (2%)
  between operations  15.3 us (2%)
    unnamed x7, waiting for transfers between devices  227 us
    reduce_scatter x1, waiting for transfers between devices, local(): lax.psum_scatter(jnp.concatenate([term_in, term_out], axis=1).reshape(sha...  105 us
    all_to_all x1, waiting for transfers between devices, sent_together(): lax.all_to_all(both, axis, split_axis=split_dim, concat_axis=concat_dim,...  68.1 us
    all_gather x1, waiting for transfers between devices, local(): lax.all_gather(proj_in, 'dp', axis=0, tiled=True)  64.8 us
    all_gather x1, waiting for transfers between devices, local(): lax.all_gather(narrow_rows, 'mp', axis=3, tiled=True)  61.7 us
    all_gather x1, waiting for transfers between devices, local(): lax.all_gather(narrow_grads, 'mp', axis=3, tiled=True)  44.2 us
    all_to_all x1, blocking collectives, sent_together(): lax.all_to_all(both, axis, split_axis=split_dim, concat_axis=concat_dim,...  38.4 us
    all_gather x1, waiting for transfers between devices, turned_gather(): out = lax.all_gather(both, axis, axis=0, tiled=True)  37.9 us
  transfers between devices with their start and end apart: 8, of which 7 were waited for; matrix products, arithmetic and copies ran while one was open for 6% of the time, Pallas kernels for 0%

commit v1 on v0

--- a/solution.py
+++ b/solution.py
@@ -1,3 +1,4 @@
+import functools
 import jax
 import jax.numpy as jnp
 from jax import lax
@@ -13,6 +14,17 @@
 WEIGHT_DECAY = 0.1
 FIRST_FIX = 1.0 - 0.9**50 * 0.9**50
 SECOND_FIX = 1.0 - 0.999**50 * 0.999**50
+
+
+def turn_target_on(u_in, peer_axis, join_dim):
+    r1 = tuple((u_in for _ in range(lax.axis_size(peer_axis))))
+    mat_out = jnp.stack(r1, axis=0)
+    clean = lax.all_to_all(mat_out, peer_axis, 0, 0)
+    placed = jnp.concatenate(clean, axis=join_dim)
+    return placed
+
+
+render_the_trees = functools.partial(turn_target_on, peer_axis="dp", join_dim=0)
 
 
 def in_blocks(value, dim, peers):
@@ -170,11 +182,7 @@
     own_experts = expert_gate.shape[0]
     total_slots = own_experts * data_parts * CAP
     expert_rows = data_parts * CAP
-    preact = jnp.dot(
-        features,
-        lax.all_gather(proj_in, "dp", axis=0, tiled=True),
-        preferred_element_type=jnp.float32,
-    )
+    preact = jnp.dot(features, render_the_trees(proj_in), preferred_element_type=jnp.float32)
     activated, gelu_slope = gelu_parts(preact)
     hidden = activated.astype(jnp.bfloat16)
     partial_value = jnp.dot(hidden, proj_out, preferred_element_type=jnp.float32)

time: 871 us -> 902 us (1.036)
  blocking collectives: 38.4 us -> 130 us
  waiting for transfers between devices: 609 us -> 543 us
    all_to_all x0 -> x1, blocking collectives: none -> 93 us  [turn_target_on(): clean = lax.all_to_all(mat_out, peer_axis, 0, 0)]
    all_gather x1 -> x0, waiting for transfers between devices: 64.8 us -> none  [local(): lax.all_gather(proj_in, 'dp', axis=0, tiled=True)]
    unnamed x7 -> x6, waiting for transfers between devices: 227 us -> 226 us
  transfers between devices with their start and end apart: 8 -> 7, of which waited for: 7 -> 6; matrix products, arithmetic and copies ran while one was open for 6% -> 6% of each run, Pallas kernels for 0% -> 0%
where the time goes in v1:
time: 902 us; the launch traced here: 899 us
  waiting for transfers between devices  543 us (60%)
  local copies, waits for them, and re-layouts  130 us (14%)
  blocking collectives  130 us (14%)
  other arithmetic  32.3 us (4%)
  matrix products  31.2 us (3%)
  starting transfers between devices  16.9 us (2%)
  between operations  15 us (2%)
    unnamed x6, waiting for transfers between devices  226 us
    reduce_scatter x1, waiting for transfers between devices, local(): lax.psum_scatter(jnp.concatenate([term_in, term_out], axis=1).reshape(sha...  105 us
    all_to_all x1, blocking collectives, turn_target_on(): clean = lax.all_to_all(mat_out, peer_axis, 0, 0)  93 us
    all_to_all x1, waiting for transfers between devices, sent_together(): lax.all_to_all(both, axis, split_axis=split_dim, concat_axis=concat_dim,...  68.1 us
    all_gather x1, waiting for transfers between devices, local(): lax.all_gather(narrow_rows, 'mp', axis=3, tiled=True)  61.8 us
    all_gather x1, waiting for transfers between devices, local(): lax.all_gather(narrow_grads, 'mp', axis=3, tiled=True)  44.2 us
    all_gather x1, waiting for transfers between devices, turned_gather(): out = lax.all_gather(both, axis, axis=0, tiled=True)  37.9 us
    all_to_all x1, blocking collectives, sent_together(): lax.all_to_all(both, axis, split_axis=split_dim, concat_axis=concat_dim,...  37.4 us
  transfers between devices with their start and end apart: 7, of which 6 were waited for; matrix products, arithmetic and copies ran while one was open for 6% of the time, Pallas kernels for 0%

profile of v1, /device:TPU:2, one launch (start us, length us, event | category | flops | bytes accessed | tf_op | source)
XLA Modules:
  0.0 898.9 jit_solution(14335757240744219276)
XLA Ops:
  8.5 93.0 %all_to_all.46 = bf16[32,144,320]{2,1,0:T(8,128)(2,1)S(1)} all-to-all(bf16[32,144,320]{2,1,0:T(8,128)(2,1)S(1)} %stack.2), channel_id=1, replica_groups=mesh['dp'=32,'mp'=8] {'dp'}, dimensions={0} | all-to-all | bytes 5898240 | tf_op jit(solution)/shard_map/all_to_all | solution.py:22
  101.6 1.4 fusion.81
  103.0 2.0 fusion.73
  105.0 6.4 all-to-all-start.1
  112.5 4.4 reduce-window.6
  121.0 3.4 scatter_custom_fusion
  125.4 5.0 gather_fusion.2
  130.4 2.5 reshape.125
  133.1 4.3 gather_fusion.1
  137.8 2.5 multiply_convert_fusion
  140.4 5.0 gather_fusion
  145.4 1.5 gather.48
  149.0 37.4 %all_to_all.47 = bf16[32,4,15,320]{3,1,2,0:T(4,128)(2,1)S(1)} all-to-all(bf16[32,4,15,320]{3,1,2,0:T(4,128)(2,1)S(1)} %copy.84), channel_id=1, replica_groups=mesh['dp'=32,'mp'=8] {'dp'}, dimensions={0} | all-to-all | bytes 2457600 | tf_op jit(solution)/shard_map/all_to_all | solution.py:44
  186.3 1.9 fusion.79
  188.2 3.6 copy.85
  191.9 2.3 copy.87
  194.5 61.8 %all-gather.4.cloned.1.call-done = bf16[1,2,480,2560]{2,1,0,3:T(2,128)(2,1)} async-done(((bf16[1,2,480,320]{2,1,0,3:T(2,128)(2,1)}), bf16[1,2,480,2560]{2,1,0,3:T(2,128)(2,1)}) %all-gather.4.cloned.1.call-update) | async-done | bytes 4915216 | tf_op jit(solution)/shard_map/all_gather | solution.py:202
  256.2 13.7 %copy.86 = bf16[1,2,480,2560]{3,2,1,0:T(8,128)(2,1)} copy(bf16[1,2,480,2560]{2,1,0,3:T(2,128)(2,1)} %all-gather.4.cloned.1.call-done) | data formatting | bytes 9830400 | tf_op jit(solution)/shard_map/all_gather | solution.py:202
  269.9 4.8 fusion.4
  275.1 2.4 fusion.2
  277.5 44.2 %all-gather.6.cloned.1.call-done = bf16[1,2,480,2560]{2,1,0,3:T(2,128)(2,1)} async-done(((bf16[1,2,480,320]{2,1,0,3:T(2,128)(2,1)}), bf16[1,2,480,2560]{2,1,0,3:T(2,128)(2,1)}) %all-gather.6.cloned.1.call-update) | async-done | bytes 4915216 | tf_op jit(solution)/shard_map/all_gather | solution.py:203
  321.8 13.8 %copy.88 = bf16[1,2,480,2560]{3,2,1,0:T(8,128)(2,1)} copy(bf16[1,2,480,2560]{2,1,0,3:T(2,128)(2,1)} %all-gather.6.cloned.1.call-done) | data formatting | bytes 9830400 | tf_op jit(solution)/shard_map/all_gather | solution.py:203
  335.5 4.0 fusion
  339.5 3.7 fusion.6
  343.3 1.5 fusion.11
  344.9 3.7 fusion.7
  348.6 8.4 pad_maximum_fusion
  357.0 26.2 %copy.89 = bf16[2,2,480,2560]{2,1,0,3:T(2,128)(2,1)} copy(bf16[2,2,480,2560]{3,2,1,0:T(8,128)(2,1)} %pad_maximum_fusion) | data formatting | bytes 19660800 | tf_op jit(solution)/shard_map/concatenate | solution.py:49
  385.1 226.2 %all-reduce.3.cloned.1.call-done = bf16[2,2,480,2560]{2,1,0,3:T(2,128)(2,1)} async-done(((bf16[2,2,480,2560]{2,1,0,3:T(2,128)(2,1)}), bf16[2,2,480,2560]{2,1,0,3:T(2,128)(2,1)}) %all-reduce.3.cloned.1.call-update) | async-done | bytes 9830416
  611.3 2.2 constant_dynamic-slice_fusion
  613.7 1.8 maximum_convert_fusion
  615.4 4.4 copy.92
  619.8 10.0 %all-to-all-start.3 = ((f32[1,4,480,320]{3,1,0,2:T(4,128)}), f32[1,4,480,320]{3,1,0,2:T(4,128)}, u32[]{:S(2)}, u32[]{:S(2)}) async-start(f32[1,4,480,320]{3,1,0,2:T(4,128)} %copy.92), calls=%async_computation.3 | async-start | bytes 5898240 | tf_op jit(solution)/shard_map/all_to_all | solution.py:44
  630.9 68.1 %all-to-all-done.3 = f32[1,4,480,320]{3,1,0,2:T(4,128)} async-done(((f32[1,4,480,320]{3,1,0,2:T(4,128)}), f32[1,4,480,320]{3,1,0,2:T(4,128)}, u32[]{:S(2)}, u32[]{:S(2)}) %all-to-all-start.3) | async-done | bytes 2457632 | tf_op jit(solution)/shard_map/all_to_all | solution.py:44
  699.0 4.0 fusion.78
  704.4 1.5 reshape.122
  710.1 1.5 reshape.121
  717.5 1.4 gather_fusion.5
  718.9 1.4 gather_fusion.10
  721.8 1.4 gather_fusion.9
  724.0 1.5 fusion.44
  726.7 37.9 %all-gather.8.cloned.1.call-done = bf16[2560,256]{1,0:T(8,128)(2,1)} async-done(((bf16[320,256]{1,0:T(8,128)(2,1)}), bf16[2560,256]{1,0:T(8,128)(2,1)}) %all-gather.8.cloned.1.call-update) | async-done | bytes 1310736 | tf_op jit(solution)/shard_map/all_gather | solution.py:61
  764.5 2.2 fusion.80
  768.0 6.9 fusion.9
  774.9 3.4 convert_bitcast_fusion
  778.3 3.0 pad_maximum_fusion.1
  783.8 105.0 %reduce-scatter.2.cloned.1.call-done = bf16[224,320]{1,0:T(8,128)(2,1)} async-done(((bf16[7168,320]{1,0:T(8,128)(2,1)}), bf16[224,320]{1,0:T(8,128)(2,1)}) %reduce-scatter.2.cloned.1.call-update) | async-done | bytes 143376 | tf_op jit(solution)/shard_map/reduce_scatter | solution.py:248
  890.7 1.7 fusion.41
  (122 shorter events, 33.7 us)
Async XLA Ops:
  7.2 328.4 %copy-start = (bf16[2,192,2560]{2,1,0:T(8,128)(2,1)S(1)}, bf16[2,192,2560]{2,1,0:T(8,128)(2,1)}, u32[]{:S(2)}) copy-start(bf16[2,192,2560]{2,1,0:T(8,128)(2,1)} %param.18) | copy-start | bytes 5898244
  8.5 93.0 %copy-start.8 = (bf16[128,4608]{1,0:T(8,128)(2,1)S(1)}, bf16[128,4608]{1,0:T(8,128)(2,1)}, u32[]{:S(2)}) copy-start(bf16[128,4608]{1,0:T(8,128)(2,1)} %param.13) | copy-start | bytes 3538948
  101.6 1.5 copy-start.7
  103.0 2.0 copy-start.12
  105.0 6.4 copy-start.22
  105.0 35.2 %all-to-all-start.1 = ((f32[8,128,320]{1,2,0:T(8,128)}), f32[8,128,320]{1,2,0:T(8,128)S(1)}, u32[]{:S(2)}, u32[]{:S(2)}) async-start(f32[8,128,320]{1,2,0:T(8,128)} %bitcast.102), calls=%async_computation.1 | async-start | bytes 2621440 | tf_op jit(solution)/shard_map/all_to_all | solution.py:37
  111.4 144.9 %all-gather.4.cloned.1.call-start = ((), (), s32[]{:S(2)}) async-start(), calls=%async_computation.5 | async-start | bytes 5898240 | tf_op jit(solution)/shard_map/all_gather | solution.py:202
  130.4 2.5 copy-start.21
  146.9 1.1 copy-start.10
  191.9 129.9 %all-gather.6.cloned.1.call-start = ((), (), s32[]{:S(2)}) async-start(), calls=%async_computation.6 | async-start | bytes 5898240 | tf_op jit(solution)/shard_map/all_gather | solution.py:203
  194.3 417.1 %all-reduce.3.cloned.1.call-start = ((), (), s32[]{:S(2)}) async-start(), calls=%async_computation.9 | async-start | bytes 20971520
  269.9 4.8 copy-start.2
  269.9 5.2 copy-start.4
  335.5 4.0 copy-start.6
  339.5 3.8 copy-start.3
  343.3 1.6 copy-start.5
  383.2 0.7 copy-start.27
  619.8 79.2 %all-to-all-start.3 = ((f32[1,4,480,320]{3,1,0,2:T(4,128)}), f32[1,4,480,320]{3,1,0,2:T(4,128)}, u32[]{:S(2)}, u32[]{:S(2)}) async-start(f32[1,4,480,320]{3,1,0,2:T(4,128)} %copy.92), calls=%async_computation.3 | async-start | bytes 5898240 | tf_op jit(solution)/shard_map/all_to_all | solution.py:44
  629.8 134.8 %all-gather.8.cloned.1.call-start = ((), (), s32[]{:S(2)}) async-start(), calls=%async_computation.7 | async-start | bytes 1474560 | tf_op jit(solution)/shard_map/all_gather | solution.py:61
  723.2 2.3 copy-start.14
  723.2 2.3 copy-start.15
  723.2 2.3 copy-start.16
  723.2 2.3 copy-start.23
  723.2 2.3 copy-start.24
  723.2 2.3 copy-start.25
  723.2 2.3 copy-start.26
  725.8 41.0 %copy-start.13 = (f32[128,320]{0,1:T(8,128)S(1)}, f32[128,320]{0,1:T(8,128)}, u32[]{:S(2)}) copy-start(f32[128,320]{0,1:T(8,128)} %copy-done.12) | copy-start | bytes 491524
  726.6 162.2 %reduce-scatter.2.cloned.1.call-start = ((), (), s32[]{:S(2)}) async-start(), calls=%async_computation.8 | async-start | bytes 5677056 | tf_op jit(solution)/shard_map/reduce_scatter | solution.py:248
  766.7 1.3 copy-start.9
  781.3 1.3 copy-start.11
  781.4 108.4 %copy-start.17 = (bf16[144,320]{1,0:T(8,128)(2,1)S(1)}, bf16[144,320]{1,0:T(8,128)(2,1)}, u32[]{:S(2)}) copy-start(bf16[144,320]{1,0:T(8,128)(2,1)} %param.14) | copy-start | bytes 276484
  781.4 108.4 %copy-start.18 = (f32[144,320]{1,0:T(8,128)S(1)}, f32[144,320]{1,0:T(8,128)}, u32[]{:S(2)}) copy-start(f32[144,320]{1,0:T(8,128)} %param.22) | copy-start | bytes 552964
  781.4 108.4 %copy-start.19 = (f32[144,320]{1,0:T(8,128)S(1)}, f32[144,320]{1,0:T(8,128)}, u32[]{:S(2)}) copy-start(f32[144,320]{1,0:T(8,128)} %param.23) | copy-start | bytes 552964
  781.4 109.3 %copy-start.20 = (f32[320,80]{0,1:T(8,128)S(1)}, f32[320,80]{0,1:T(8,128)}, u32[]{:S(2)}) copy-start(f32[320,80]{0,1:T(8,128)} %param.24) | copy-start | bytes 307204
  782.5 109.8 %copy-start.1 = (bf16[2,192,2560]{2,1,0:T(8,128)(2,1)S(1)}, bf16[2,192,2560]{2,1,0:T(8,128)(2,1)}, u32[]{:S(2)}) copy-start(bf16[2,192,2560]{2,1,0:T(8,128)(2,1)} %param.18) | copy-start | bytes 5898244
Sparse Core Ops, SparseCore 0:
  192.0 64.1 all-gather.3
  258.0 63.6 all-gather.5
  383.4 227.8 all-reduce.2
  726.8 37.7 all-gather.7
  781.5 107.2 reduce-scatter.1
